TPU v7x, 32 devices: a whole 2x2x4 slice. The times are simulated.
32 devices in a mesh: gx: 4 (over y, x), gy: 2 (over core), gz: 4 (over z).
Axes of the slice: x: 2, y: 2, z: 4, core: 2. Of those that a mesh axis runs over, the one named last changes fastest.
Arguments:
- positions: float32 [3, 8, 8, 8, 128], P(None, 'gx', 'gy', 'gz'), may hold values from 0 to 1
- type_ids: int32 [8, 8, 8, 128], P('gx', 'gy', 'gz'), may hold values from 0 to 1
- counts: int32 [8, 8, 8], P('gx', 'gy', 'gz'), may hold values from 64 to 128
- type_charge: float32 [2], replicated, may hold values from -1 to 1
- type_sigma: float32 [2], replicated, may hold values from 0.2 to 0.35
- type_epsilon: float32 [2], replicated, may hold values from 0.05 to 0.5
Outputs:
- forces: float32 [3, 8, 8, 8, 128], P(None, 'gx', 'gy', 'gz')
- totals: float32 [2], replicated
All inputs are finite; a program needn't handle non-finite values.
Results may differ from a plain program's by a relative error of at most 0.0003.
Values sent between devices are 32-bit elements; how exact they have to be, the bound alone decides.
A program may use at most 64 MiB of HBM per device.

v0:
```python
import jax
import jax.numpy as jnp
from jax import lax
from jax.sharding import PartitionSpec as P

soft_core = 0.09
corner_pairs = [
    (first_corner, second_corner)
    for first_corner in range(8)
    for second_corner in range(8)
    if first_corner & second_corner == 0 and first_corner <= second_corner
]


def passed_along(value, axis, steps):
    count = lax.axis_size(axis)
    pairs = [(source, (source + steps) % count) for source in range(count)]
    return lax.ppermute(value, axis, pairs)


def corner_of(which):
    return (which & 1, which >> 1 & 1, which >> 2 & 1)


def atom_table(positions, type_ids, counts, type_charge, type_sigma, type_epsilon):
    type_count = type_charge.shape[0]
    kinds_shape = (type_count, 1, 1, 1, 1)
    onehot = (
        type_ids[None] == jnp.arange(type_count, dtype=jnp.int32).reshape(kinds_shape)
    ).astype(jnp.float32)
    charge = jnp.sum(onehot * type_charge.reshape(kinds_shape), 0)
    sigma_atom = jnp.sum(onehot * type_sigma.reshape(kinds_shape), 0)
    depth_atom = jnp.sum(onehot * jnp.sqrt(type_epsilon).reshape(kinds_shape), 0)
    slots = lax.broadcasted_iota(jnp.int32, type_ids.shape, 3)
    occupied = (slots < counts[..., None]).astype(jnp.float32)
    return jnp.stack(
        [positions[0], positions[1], positions[2], charge, sigma_atom, depth_atom, occupied]
    )


def pair_terms(first, second, offset, selfpair):
    displace = second[:3, :, None, :] - first[:3, :, :, None] + offset[:, None, None, None]
    dist_sq = jnp.sum(displace * displace, 0)
    width_atoms = first.shape[-1]
    live_mask = first[6][:, :, None] * second[6][:, None, :] * (dist_sq < 1.0).astype(jnp.float32)
    if selfpair:
        ordered = (
            lax.broadcasted_iota(jnp.int32, (width_atoms, width_atoms), 0)
            < lax.broadcasted_iota(jnp.int32, (width_atoms, width_atoms), 1)
        ).astype(jnp.float32)
        live_mask = live_mask * ordered[None]
    sigma_pair = 0.5 * (first[4][:, :, None] + second[4][:, None, :])
    depth_pair = first[5][:, :, None] * second[5][:, None, :]
    coulomb = first[3][:, :, None] * second[3][:, None, :]
    soft_sq = dist_sq + soft_core
    inverse = lax.rsqrt(soft_sq)
    ratio_six = (sigma_pair * sigma_pair / soft_sq) ** 3
    ratio_twelve = ratio_six * ratio_six
    value_here = 4.0 * depth_pair * (ratio_twelve - ratio_six) + coulomb * inverse
    slope_here = (
        4.0 * depth_pair * (6.0 * ratio_six - 12.0 * ratio_twelve) - coulomb * inverse
    ) * inverse
    cut_sq = 1.0 + soft_core
    cut_len = cut_sq**0.5
    cut_six = (sigma_pair * sigma_pair / cut_sq) ** 3
    cut_twelve = cut_six * cut_six
    value_cut = 4.0 * depth_pair * (cut_twelve - cut_six) + coulomb / cut_len
    slope_cut = (
        4.0 * depth_pair * (6.0 * cut_six - 12.0 * cut_twelve) - coulomb / cut_len
    ) / cut_len
    energy = live_mask * (value_here - value_cut - (soft_sq * inverse - cut_len) * slope_cut)
    slope = live_mask * (slope_here - slope_cut) * inverse
    weighted = slope[None] * displace
    return (jnp.sum(weighted, 3), -jnp.sum(weighted, 2), jnp.sum(energy), jnp.sum(slope * dist_sq))


def per_device(positions, type_ids, counts, type_charge, type_sigma, type_epsilon):
    features = atom_table(positions, type_ids, counts, type_charge, type_sigma, type_epsilon)
    size_x, size_y, size_z, width_atoms = features.shape[1:]
    extended = jnp.concatenate([features, passed_along(features[:, :1], "gx", -1)], 1)
    extended = jnp.concatenate([extended, passed_along(extended[:, :, :1], "gy", -1)], 2)
    extended = jnp.concatenate([extended, passed_along(extended[:, :, :, :1], "gz", -1)], 3)
    cell_rows = size_x * size_y * size_z

    def slabs_of(which):
        shift_x, shift_y, shift_z = corner_of(which)
        view = extended[
            :, shift_x : shift_x + size_x, shift_y : shift_y + size_y, shift_z : shift_z + size_z
        ]
        return view.reshape((7, cell_rows, width_atoms))

    reaction = jnp.zeros((3, size_x + 1, size_y + 1, size_z + 1, width_atoms), jnp.float32)

    def deposit(reaction, force_rows, which):
        shift_x, shift_y, shift_z = corner_of(which)
        grid = force_rows.reshape((3, size_x, size_y, size_z, width_atoms))
        return reaction.at[
            :, shift_x : shift_x + size_x, shift_y : shift_y + size_y, shift_z : shift_z + size_z
        ].add(grid)

    energy = jnp.float32(0.0)
    virial = jnp.float32(0.0)
    for first_corner, second_corner in corner_pairs:
        offset = jnp.array(
            [float(a - b) for a, b in zip(corner_of(second_corner), corner_of(first_corner))],
            jnp.float32,
        )
        selfpair = first_corner == second_corner
        force_first, force_second, energies, virials = pair_terms(
            slabs_of(first_corner), slabs_of(second_corner), offset, selfpair
        )
        reaction = deposit(reaction, force_first, first_corner)
        reaction = deposit(reaction, force_second, second_corner)
        energy = energy + energies
        virial = virial + virials
    returned = passed_along(reaction[:, :, :, size_z:], "gz", 1)
    reaction = reaction[:, :, :, :size_z].at[:, :, :, :1].add(returned)
    returned = passed_along(reaction[:, :, size_y:], "gy", 1)
    reaction = reaction[:, :, :size_y].at[:, :, :1].add(returned)
    returned = passed_along(reaction[:, size_x:], "gx", 1)
    forces = reaction[:, :size_x].at[:, :1].add(returned)
    summed = lax.psum((energy, virial), ("gx", "gy", "gz"))
    normaliser = 1.0 / (
        size_x
        * lax.axis_size("gx")
        * size_y
        * lax.axis_size("gy")
        * size_z
        * lax.axis_size("gz")
        * width_atoms
    )
    totals = jnp.stack([summed[0], summed[1]]) * normaliser
    return (forces, totals)


def solution(mesh):
    in_specs = (
        P(None, "gx", "gy", "gz", None),
        P("gx", "gy", "gz", None),
        P("gx", "gy", "gz"),
        P(),
        P(),
        P(),
    )
    out_specs = (P(None, "gx", "gy", "gz", None), P())
    return jax.shard_map(
        per_device, mesh=mesh, in_specs=in_specs, out_specs=out_specs, check_vma=False
    )
```

profile of v0, /device:TPU:12, one launch (start us, length us, event | category | flops | bytes accessed | tf_op | source)
XLA Modules:
  0.0 161.7 jit_solution(2301316743114900686)
XLA Ops:
  0.7 0.7 copy.33
  1.4 0.7 sqrt.3
  2.1 0.7 constant_dynamic-update-slice_fusion.4
  2.8 0.8 copy.32
  3.6 0.8 select_reduce_fusion.2
  4.4 0.1 constant_dynamic-update-slice_fusion
  4.5 1.5 collective-permute-start
  6.0 0.1 lt.135
  6.1 0.1 fusion.332
  6.2 2.2 %collective-permute-done = f32[7,1,4,2,128]{4,3,2,1,0:T(2,128)S(1)} collective-permute-done((f32[7,1,4,2,128]{4,3,2,1,0:T(2,128)S(1)}, f32[7,1,4,2,128]{4,3,2,1,0:T(2,128)S(1)}, u32[]{:S(2)}, u32[]{:S(2)}) %collective-permute-start) | collective-permute-done | bytes 28704 | tf_op jit(solution)/shard_map/ppermute | solution.py:18
  8.4 0.1 collective-permute-start.1
  8.5 1.2 collective-permute-done.1
  9.8 0.5 collective-permute-start.2
  10.3 3.7 %collective-permute-done.2 = f32[7,3,5,1,128]{4,3,2,1,0:T(1,128)S(1)} collective-permute-done((f32[7,3,5,1,128]{4,3,2,1,0:T(1,128)S(1)}, f32[7,3,5,1,128]{4,3,2,1,0:T(1,128)S(1)}, u32[]{:S(2)}, u32[]{:S(2)}) %collective-permute-start.2) | collective-permute-done | bytes 53792 | tf_op jit(solution)/shard_map/ppermute | solution.py:18
  14.0 0.1 pad_maximum_fusion
  14.3 3.5 %multiply_reduce_fusion.1 = (f32[16,128,128]{2,1,0:T(8,128)S(1)}, f32[16,128,128]{2,1,0:T(8,128)S(1)}, f32[16,128,128]{2,1,0:T(8,128)S(1)}, f32[16,128,128]{2,1,0:T(8,128)S(1)}, f32[16,128,128]{2,1,0:T(8,128)S(1)}) fusion(f32[3]{0:T(128)S(1)} %copy-done.15, f32[3,16,128]{2,1,0:T(8,128)S(1)} %bitcast.72, f32[3,16,128]{2,1,0:T(8,128)S(1)} %bitcast.112, ...), kind=kLoop, calls=%fused_computation.10 | loop fusion | flops 14417920 | bytes 5341244 | tf_op jit(solution)/shard_map/reduce_sum | solution.py:43
  17.7 3.1 %fusion.132 = (f32[]{:T(128)}, f32[]{:T(128)}, f32[16,128,128]{2,1,0:T(8,128)S(1)}) fusion(f32[16,128,128]{2,1,0:T(8,128)S(1)} %get-tuple-element.475, f32[16,128]{1,0:T(8,128)S(1)} %bitcast.114, f32[16,128]{1,0:T(8,128)S(1)} %bitcast.138, f32[16,128]{1,0:T(8,128)S(1)} %bitcast.135, f32[16,128]{1,0:T(8,128)S(1)} %bitcast.132, f32[16,128]{1,0:T(8,128)S(1)} %bitcast.123, ...), kind=kLoop, calls=%fused_computation.314 | loop fusion | flops 13107198 | bytes 2162696 | tf_op jit(solution)/shard_map/reduce_sum | solution.py:74
  21.0 7.4 %fusion.160 = (f32[]{:T(128)}, f32[]{:T(128)}, f32[]{:T(128)}, f32[]{:T(128)}, f32[]{:T(128)}, /*index=5*/f32[]{:T(128)}, f32[16,128,128]{2,1,0:T(8,128)S(1)}, f32[16,128,128]{2,1,0:T(8,128)S(1)}, f32[16,128,128]{2,1,0:T(8,128)S(1)}) fusion(f32[16,128,128]{2,1,0:T(8,128)S(1)} %get-tuple-element.471, f32[16,128]{1,0:T(8,128)S(1)} %bitcast.124, ...), kind=kLoop, calls=%fused_computation.342 | loop fusion | flops 39321596 | bytes 6389784 | tf_op jit(solution)/shard_map/reduce_sum | solution.py:74
  28.4 8.2 %multiply_reduce_fusion = (f32[16,128,128]{2,1,0:T(8,128)S(1)}, f32[16,128,128]{2,1,0:T(8,128)S(1)}, f32[3,16,128]{2,1,0:T(8,128)}, f32[3,16,128]{2,1,0:T(8,128)...) fusion(f32[3]{0:T(128)S(1)} %copy-done.11, ...), kind=kLoop, calls=%fused_computation.5 | loop fusion | flops 29061120 | bytes 9756780 | tf_op jit(solution)/shard_map/reduce_sum | solution.py:43
  36.7 7.4 %fusion.146 = (f32[]{:T(128)}, f32[]{:T(128)}, f32[]{:T(128)}, f32[]{:T(128)}, f32[]{:T(128)}, /*index=5*/f32[]{:T(128)}, f32[16,128,128]{2,1,0:T(8,128)S(1)}, f32[16,128,128]{2,1,0:T(8,128)S(1)}, f32[16,128,128]{2,1,0:T(8,128)S(1)}) fusion(f32[16,128,128]{2,1,0:T(8,128)S(1)} %get-tuple-element.470, f32[16,128]{1,0:T(8,128)S(1)} %bitcast.115, ...), kind=kLoop, calls=%fused_computation.328 | loop fusion | flops 39321596 | bytes 6389784 | tf_op jit(solution)/shard_map/reduce_sum | solution.py:74
  44.1 4.8 %rsqrt_multiply_fusion.31 = (f32[16,128,128]{2,1,0:T(8,128)S(1)}, f32[16,128,128]{2,1,0:T(8,128)S(1)}, f32[16,128,128]{2,1,0:T(8,128)S(1)}) fusion(f32[16,128,128]{2,1,0:T(8,128)S(1)} %get-tuple-element.468, f32[16,128]{1,0:T(8,128)S(1)} %bitcast.147, f32[16,128]{1,0:T(8,128)S(1)} %bitcast.144, f32[16,128]{1,0:T(8,128)S(1)} %bitcast.141, ...), kind=kLoop, calls=%fused_computation.241 | loop fusion | flops 27525120 | bytes 6389760 | tf_op jit(solution)/shard_map/mul | solution.py:72
  48.9 10.2 %fusion.4 = (f32[3,16,128]{2,1,0:T(8,128)S(1)}, f32[3,16,128]{2,1,0:T(8,128)S(1)}, f32[16,128,128]{2,1,0:T(8,128)S(1)}, f32[3,16,128]{2,1,0:T(8,128)S(1)}, f32[3...) fusion(f32[16,128,128]{2,1,0:T(8,128)S(1)} %get-tuple-element.5, ...), kind=kLoop, calls=%fused_computation.8 | loop fusion | flops 31383552 | bytes 9879636 | tf_op jit(solution)/shard_map/reduce_sum | solution.py:74
  59.2 4.9 %fusion.167 = (f32[]{:T(128)}, f32[]{:T(128)}, f32[]{:T(128)}, f32[]{:T(128)}, f32[16,128,128]{2,1,0:T(8,128)S(1)}) fusion(f32[16,128,128]{2,1,0:T(8,128)S(1)} %get-tuple-element.459, f32[16,128]{1,0:T(8,128)S(1)} %bitcast.148, f32[16,128]{1,0:T(8,128)S(1)} %bitcast.145, f32[16,128]{1,0:T(8,128)S(1)} %bitcast.142, f32[16,128]{1,0:T(8,128)S(1)} %bitcast.130, ...), kind=kLoop, calls=%fused_computation.349 | loop fusion | flops 23855100 | bytes 4292624 | tf_op jit(solution)/shard_map/reduce_sum | solution.py:74
  64.1 7.0 %fusion.153 = (f32[]{:T(128)}, f32[]{:T(128)}, f32[]{:T(128)}, f32[]{:T(128)}, f32[]{:T(128)}, /*index=5*/f32[]{:T(128)}, f32[16,128,128]{2,1,0:T(8,128)S(1)}, f32[16,128,128]{2,1,0:T(8,128)S(1)}) fusion(f32[16,128,128]{2,1,0:T(8,128)S(1)} %get-tuple-element.460, f32[16,128]{1,0:T(8,128)S(1)} %bitcast.125, f32[16,128]{1,0:T(8,128)S(1)} %bitcast.122, ...), kind=kLoop, calls=%fused_computation.335 | loop fusion | flops 37224444 | bytes 6455320 | tf_op jit(solution)/shard_map/reduce_sum | solution.py:74
  71.1 4.6 %fusion.125 = (f32[]{:T(128)}, f32[]{:T(128)}, f32[]{:T(128)}, f32[]{:T(128)}, f32[16,128,128]{2,1,0:T(8,128)S(1)}) fusion(f32[16,128,128]{2,1,0:T(8,128)S(1)} %get-tuple-element.457, f32[16,128]{1,0:T(8,128)S(1)} %bitcast.192, f32[16,128]{1,0:T(8,128)S(1)} %bitcast.193, f32[16,128]{1,0:T(8,128)S(1)} %bitcast.194, f32[16,128]{1,0:T(8,128)S(1)} %bitcast.191, ...), kind=kLoop, calls=%fused_computation.307 | loop fusion | flops 23855100 | bytes 4292624 | tf_op jit(solution)/shard_map/reduce_sum | solution.py:74
  75.7 3.1 %fusion.22 = (f32[3,16,128]{2,1,0:T(8,128)S(1)}, f32[3,16,128]{2,1,0:T(8,128)S(1)}, f32[3,16,128]{2,1,0:T(8,128)S(1)}, f32[3,16,128]{2,1,0:T(8,128)S(1)}) fusion(f32[16,128,128]{2,1,0:T(8,128)S(1)} %get-tuple-element.489, f32[3,16,128]{2,1,0:T(8,128)S(1)} %bitcast.107, f32[3,16,128]{2,1,0:T(8,128)S(1)} %bitcast.82, f32[16,128,128]{2,1,0:T(8,128)S(1)} %get-tuple-element.497), kind=kLoop, calls=%fused_computation.38 | loop fusion | flops 7053312 | bytes 2244608 | tf_op jit(solution)/shard_map/reduce_sum | solution.py:74
  78.9 0.6 neg.108
  79.8 0.2 scatter-add.119
  80.0 0.8 fusion.319
  80.8 0.8 slice_add_fusion.16
  81.5 0.2 scatter-add.121
  81.8 0.2 scatter-add.125
  82.1 0.2 scatter-add.129
  82.4 5.0 %fusion.10 = (f32[3,16,128]{2,1,0:T(8,128)S(1)}, f32[3,16,128]{2,1,0:T(8,128)S(1)}, f32[3,16,128]{2,1,0:T(8,128)S(1)}, f32[3,16,128]{2,1,0:T(8,128)S(1)}, f32[3,...) fusion(f32[16,128,128]{2,1,0:T(8,128)S(1)} %get-tuple-element.496, f32[3]{0:T(128)S(1)} %copy-done.12, ...), kind=kLoop, calls=%fused_computation.18 | loop fusion | flops 11759616 | bytes 3366948 | tf_op jit(solution)/shard_map/reduce_sum | solution.py:74
  87.5 0.2 scatter-add.135
  87.8 0.2 scatter-add.139
  88.1 0.2 scatter-add.141
  88.4 0.2 scatter-add.145
  88.7 0.2 scatter-add.149
  89.0 1.6 %collective-permute-start.3 = (f32[3,3,5,1,128]{4,3,2,1,0:T(1,128)S(1)}, f32[3,3,5,1,128]{4,3,2,1,0:T(1,128)S(1)}, u32[]{:S(2)}, u32[]{:S(2)}) collective-permute-start(f32[3,3,5,1,128]{4,3,2,1,0:T(1,128)S(1)} %slice.1705), channel_id=1, source_target_pairs={{0,1},{1,2},{2,3},{3,0},{4,5},{5,6},{6,7},{7,4},{8,9},{9,10},{10,1... | collective-permute-start | bytes 69128 | tf_op jit(solution)/shard_map/ppermute | solution.py:18
  90.6 2.2 %collective-permute-done.3 = f32[3,3,5,1,128]{4,3,2,1,0:T(1,128)S(1)} collective-permute-done((f32[3,3,5,1,128]{4,3,2,1,0:T(1,128)S(1)}, f32[3,3,5,1,128]{4,3,2,1,0:T(1,128)S(1)}, u32[]{:S(2)}, u32[]{:S(2)}) %collective-permute-start.3) | collective-permute-done | bytes 23072 | tf_op jit(solution)/shard_map/ppermute | solution.py:18
  92.8 0.1 scatter-add.150
  93.0 0.1 collective-permute-start.4
  110.7 45.7 %all-reduce.1 = (f32[1]{0:T(128)}, f32[1]{0:T(128)}) all-reduce(f32[1]{0:T(128)} %bitcast.71, f32[1]{0:T(128)} %bitcast.70), channel_id=1, replica_groups=mesh['gx'=4,'gy'=2,'gz'=4] {'gx','gy','gz'}, use_global_device_ids=true, to_apply=%region_74.0 | all-reduce | flops 2 | bytes 16 | tf_op jit(solution)/shard_map/psum | solution.py:122
  156.4 0.6 collective-permute-start.5
  157.0 1.9 %maximum_multiply_fusion = f32[2]{0:T(128)} fusion(f32[1]{0:T(128)} %get-tuple-element.485, f32[1]{0:T(128)} %get-tuple-element.486), kind=kLoop, calls=%fused_computation.665 | loop fusion | flops 4 | bytes 16 | tf_op jit(solution)/shard_map/mul | solution.py:132
  159.0 2.1 %collective-permute-done.5 = f32[3,1,4,2,128]{4,3,2,1,0:T(2,128)S(1)} collective-permute-done((f32[3,1,4,2,128]{4,3,2,1,0:T(2,128)S(1)}, f32[3,1,4,2,128]{4,3,2,1,0:T(2,128)S(1)}, u32[]{:S(2)}, u32[]{:S(2)}) %collective-permute-start.5) | collective-permute-done | bytes 12320 | tf_op jit(solution)/shard_map/ppermute | solution.py:18
  161.1 0.6 copy-done.3
  (100 shorter events, 1.3 us)
Async XLA Ops:
  0.6 13.6 %copy-start.5 = (f32[3]{0:T(128)S(1)}, f32[3]{0:T(128)}, u32[]{:S(2)}) copy-start(f32[3]{0:T(128)} %constant.879.clone) | copy-start | bytes 40
  0.6 13.6 %copy-start.13 = (f32[3]{0:T(128)S(1)}, f32[3]{0:T(128)}, u32[]{:S(2)}) copy-start(f32[3]{0:T(128)} %constant.880.clone) | copy-start | bytes 40
  0.7 13.6 %copy-start.14 = (f32[3]{0:T(128)S(1)}, f32[3]{0:T(128)}, u32[]{:S(2)}) copy-start(f32[3]{0:T(128)} %constant.883.clone) | copy-start | bytes 40
  0.7 13.6 %copy-start.6 = (f32[3]{0:T(128)S(1)}, f32[3]{0:T(128)}, u32[]{:S(2)}) copy-start(f32[3]{0:T(128)} %constant.886.clone) | copy-start | bytes 40
  0.7 13.6 %copy-start.15 = (f32[3]{0:T(128)S(1)}, f32[3]{0:T(128)}, u32[]{:S(2)}) copy-start(f32[3]{0:T(128)} %constant.890.clone) | copy-start | bytes 40
  0.7 13.6 %copy-start = (f32[3,2,4,2,128]{4,3,2,1,0:T(2,128)S(1)}, f32[3,2,4,2,128]{4,3,2,1,0:T(2,128)}, u32[]{:S(2)}) copy-start(f32[3,2,4,2,128]{4,3,2,1,0:T(2,128)} %param.82) | copy-start | bytes 73732
  4.5 3.9 %collective-permute-start = (f32[7,1,4,2,128]{4,3,2,1,0:T(2,128)S(1)}, f32[7,1,4,2,128]{4,3,2,1,0:T(2,128)S(1)}, u32[]{:S(2)}, u32[]{:S(2)}) collective-permute-start(f32[7,1,4,2,128]{4,3,2,1,0:T(2,128)S(1)} %slice.1661), channel_id=1, source_target_pairs={{0,24},{8,0},{16,8},{24,16},{1,25},{9,1},{17,9},{25,17},{2,26},{10... | collective-permute-start | bytes 86024 | tf_op jit(solution)/shard_map/ppermute | solution.py:18
  8.4 1.3 collective-permute-start.1
  9.8 4.2 %collective-permute-start.2 = (f32[7,3,5,1,128]{4,3,2,1,0:T(1,128)S(1)}, f32[7,3,5,1,128]{4,3,2,1,0:T(1,128)S(1)}, u32[]{:S(2)}, u32[]{:S(2)}) collective-permute-start(f32[7,3,5,1,128]{4,3,2,1,0:T(1,128)S(1)} %slice.1680), channel_id=1, source_target_pairs={{0,3},{1,0},{2,1},{3,2},{4,7},{5,4},{6,5},{7,6},{8,11},{9,8},{10,9... | collective-permute-start | bytes 161288 | tf_op jit(solution)/shard_map/ppermute | solution.py:18
  20.9 7.5 %copy-start.7 = (f32[3]{0:T(128)S(1)}, f32[3]{0:T(128)}, u32[]{:S(2)}) copy-start(f32[3]{0:T(128)} %constant.881.clone) | copy-start | bytes 40
  20.9 7.5 %copy-start.8 = (f32[3]{0:T(128)S(1)}, f32[3]{0:T(128)}, u32[]{:S(2)}) copy-start(f32[3]{0:T(128)} %constant.882.clone) | copy-start | bytes 40
  20.9 7.5 %copy-start.9 = (f32[3]{0:T(128)S(1)}, f32[3]{0:T(128)}, u32[]{:S(2)}) copy-start(f32[3]{0:T(128)} %constant.884.clone) | copy-start | bytes 40
  20.9 7.4 %copy-start.10 = (f32[3]{0:T(128)S(1)}, f32[3]{0:T(128)}, u32[]{:S(2)}) copy-start(f32[3]{0:T(128)} %constant.888.clone) | copy-start | bytes 40
  21.0 7.4 %copy-start.11 = (f32[3]{0:T(128)S(1)}, f32[3]{0:T(128)}, u32[]{:S(2)}) copy-start(f32[3]{0:T(128)} %constant.891.clone) | copy-start | bytes 40
  21.0 7.4 %copy-start.12 = (f32[3]{0:T(128)S(1)}, f32[3]{0:T(128)}, u32[]{:S(2)}) copy-start(f32[3]{0:T(128)} %constant.889.clone) | copy-start | bytes 40
  44.1 4.8 %copy-start.4 = (f32[3]{0:T(128)S(1)}, f32[3]{0:T(128)}, u32[]{:S(2)}) copy-start(f32[3]{0:T(128)} %constant.887.clone) | copy-start | bytes 40
  82.3 6.0 %copy-start.1 = (f32[3,16,128]{2,1,0:T(8,128)S(1)}, f32[3,16,128]{2,1,0:T(8,128)}, u32[]{:S(2)}) copy-start(f32[3,16,128]{2,1,0:T(8,128)} %get-tuple-element.462) | copy-start | bytes 73732
  82.3 6.0 %copy-start.2 = (f32[3,16,128]{2,1,0:T(8,128)S(1)}, f32[3,16,128]{2,1,0:T(8,128)}, u32[]{:S(2)}) copy-start(f32[3,16,128]{2,1,0:T(8,128)} %get-tuple-element.461) | copy-start | bytes 73732
  89.0 3.9 %collective-permute-start.3 = (f32[3,3,5,1,128]{4,3,2,1,0:T(1,128)S(1)}, f32[3,3,5,1,128]{4,3,2,1,0:T(1,128)S(1)}, u32[]{:S(2)}, u32[]{:S(2)}) collective-permute-start(f32[3,3,5,1,128]{4,3,2,1,0:T(1,128)S(1)} %slice.1705), channel_id=1, source_target_pairs={{0,1},{1,2},{2,3},{3,0},{4,5},{5,6},{6,7},{7,4},{8,9},{9,10},{10,1... | collective-permute-start | bytes 69128 | tf_op jit(solution)/shard_map/ppermute | solution.py:18
  93.0 63.4 %collective-permute-start.4 = (f32[3,3,1,2,128]{4,3,2,1,0:T(2,128)S(1)}, f32[3,3,1,2,128]{4,3,2,1,0:T(2,128)S(1)}, u32[]{:S(2)}, u32[]{:S(2)}) collective-permute-start(f32[3,3,1,2,128]{4,3,2,1,0:T(2,128)S(1)} %slice.1708), channel_id=1, source_target_pairs={{0,4},{4,0},{1,5},{5,1},{2,6},{6,2},{3,7},{7,3},{8,12},{12,8},{9,1... | collective-permute-start | bytes 27656 | tf_op jit(solution)/shard_map/ppermute | solution.py:18
  156.4 4.6 %collective-permute-start.5 = (f32[3,1,4,2,128]{4,3,2,1,0:T(2,128)S(1)}, f32[3,1,4,2,128]{4,3,2,1,0:T(2,128)S(1)}, u32[]{:S(2)}, u32[]{:S(2)}) collective-permute-start(f32[3,1,4,2,128]{4,3,2,1,0:T(2,128)S(1)} %slice.1711), channel_id=1, source_target_pairs={{0,8},{8,16},{16,24},{24,0},{1,9},{9,17},{17,25},{25,1},{2,10},{10... | collective-permute-start | bytes 36872 | tf_op jit(solution)/shard_map/ppermute | solution.py:18
  161.1 0.6 copy-start.3
where the time goes:
time: 162 us
  other arithmetic  75.3 us (46%)
  blocking collectives  45.7 us (28%)
  between operations  19 us (12%)
  waiting for transfers between devices  11.4 us (7%)
  local copies, waits for them, and re-layouts  5.94 us (4%)
  starting transfers between devices  4.34 us (3%)
    psum x1, blocking collectives, per_device(): summed = lax.psum((energy, virial), ('gx', 'gy', 'gz'))  45.7 us
    reduce_sum x6, other arithmetic, pair_terms(): jnp.sum(energy)  34.4 us
    reduce_sum x3, other arithmetic, pair_terms(): jnp.sum(weighted, 2)  18.3 us
    reduce_sum x2, other arithmetic, pair_terms(): dist_sq = jnp.sum(displace * displace, 0)  11.7 us
    ppermute x6, waiting for transfers between devices, passed_along(): return lax.ppermute(value, axis, pairs)  11.4 us
    mul x1, other arithmetic, pair_terms(): slope = live_mask * (slope_here - slope_cut) * inverse  4.8 us
    ppermute x6, starting transfers between devices, passed_along(): return lax.ppermute(value, axis, pairs)  4.34 us
  transfers between devices with their start and end apart: 6, of which 5 were waited for; matrix products, arithmetic and copies ran while one was open for 1% of the time, Pallas kernels for 0%

commit v1 on v0

--- a/solution.py
+++ b/solution.py
@@ -119,7 +119,9 @@
     reaction = reaction[:, :, :size_y].at[:, :, :1].add(returned)
     returned = passed_along(reaction[:, size_x:], "gx", 1)
     forces = reaction[:, :size_x].at[:, :1].add(returned)
-    summed = lax.psum((energy, virial), ("gx", "gy", "gz"))
+    summed = (energy, virial)
+    for i in (("gy", "gz"), "gx"):
+        summed = lax.psum(summed, i)
     normaliser = 1.0 / (
         size_x
         * lax.axis_size("gx")

time: 162 us -> 149 us (0.920)
  the two profiles are of different devices: /device:TPU:12 before, /device:TPU:0 now
where the time goes in v1:
time: 149 us; the launch traced here: 148 us
  other arithmetic  74.8 us (50%)
  blocking collectives  27.7 us (19%)
  between operations  19 us (13%)
  waiting for transfers between devices  12.5 us (8%)
  starting transfers between devices  8.2 us (6%)
  local copies, waits for them, and re-layouts  5.94 us (4%)
    reduce_sum x6, other arithmetic, pair_terms(): jnp.sum(energy)  34.4 us
    psum x2, blocking collectives, per_device(): summed = lax.psum(summed, i)  27.7 us
    reduce_sum x3, other arithmetic, pair_terms(): jnp.sum(weighted, 2)  17.9 us
    ppermute x6, waiting for transfers between devices, passed_along(): return lax.ppermute(value, axis, pairs)  12.5 us
    reduce_sum x2, other arithmetic, pair_terms(): dist_sq = jnp.sum(displace * displace, 0)  11.7 us
    ppermute x6, starting transfers between devices, passed_along(): return lax.ppermute(value, axis, pairs)  8.2 us
    mul x1, other arithmetic, pair_terms(): slope = live_mask * (slope_here - slope_cut) * inverse  4.81 us
  transfers between devices with their start and end apart: 6, of which 5 were waited for; matrix products, arithmetic and copies ran while one was open for 1% of the time, Pallas kernels for 0%

profile of v1, /device:TPU:0, one launch (start us, length us, event | category | flops | bytes accessed | tf_op | source)
XLA Modules:
  0.0 148.2 jit_solution(9565236788531744549)
XLA Ops:
  0.7 0.7 copy.33
  1.4 0.7 sqrt.3
  2.1 0.7 constant_dynamic-update-slice_fusion.4
  2.8 0.8 copy.32
  3.6 0.8 select_reduce_fusion.2
  4.4 0.1 constant_dynamic-update-slice_fusion
  4.5 4.0 %collective-permute-start = (f32[7,1,4,2,128]{4,3,2,1,0:T(2,128)S(1)}, f32[7,1,4,2,128]{4,3,2,1,0:T(2,128)S(1)}, u32[]{:S(2)}, u32[]{:S(2)}) collective-permute-start(f32[7,1,4,2,128]{4,3,2,1,0:T(2,128)S(1)} %slice.1661), channel_id=1, source_target_pairs={{0,24},{8,0},{16,8},{24,16},{1,25},{9,1},{17,9},{25,17},{2,26},{10... | collective-permute-start | bytes 86024 | tf_op jit(solution)/shard_map/ppermute | solution.py:18
  8.5 0.1 lt.135
  8.6 0.1 fusion.332
  8.7 1.3 collective-permute-done
  10.1 0.1 collective-permute-start.1
  10.2 1.2 collective-permute-done.1
  11.4 3.7 %collective-permute-start.2 = (f32[7,3,5,1,128]{4,3,2,1,0:T(1,128)S(1)}, f32[7,3,5,1,128]{4,3,2,1,0:T(1,128)S(1)}, u32[]{:S(2)}, u32[]{:S(2)}) collective-permute-start(f32[7,3,5,1,128]{4,3,2,1,0:T(1,128)S(1)} %slice.1680), channel_id=1, source_target_pairs={{0,3},{1,0},{2,1},{3,2},{4,7},{5,4},{6,5},{7,6},{8,11},{9,8},{10,9... | collective-permute-start | bytes 161288 | tf_op jit(solution)/shard_map/ppermute | solution.py:18
  15.1 1.8 %collective-permute-done.2 = f32[7,3,5,1,128]{4,3,2,1,0:T(1,128)S(1)} collective-permute-done((f32[7,3,5,1,128]{4,3,2,1,0:T(1,128)S(1)}, f32[7,3,5,1,128]{4,3,2,1,0:T(1,128)S(1)}, u32[]{:S(2)}, u32[]{:S(2)}) %collective-permute-start.2) | collective-permute-done | bytes 53792 | tf_op jit(solution)/shard_map/ppermute | solution.py:18
  16.9 0.1 pad_maximum_fusion
  17.1 3.5 %multiply_reduce_fusion.1 = (f32[16,128,128]{2,1,0:T(8,128)S(1)}, f32[16,128,128]{2,1,0:T(8,128)S(1)}, f32[16,128,128]{2,1,0:T(8,128)S(1)}, f32[16,128,128]{2,1,0:T(8,128)S(1)}, f32[16,128,128]{2,1,0:T(8,128)S(1)}) fusion(f32[3]{0:T(128)S(1)} %copy-done.15, f32[3,16,128]{2,1,0:T(8,128)S(1)} %bitcast.72, f32[3,16,128]{2,1,0:T(8,128)S(1)} %bitcast.112, ...), kind=kLoop, calls=%fused_computation.10 | loop fusion | flops 14417920 | bytes 5341244 | tf_op jit(solution)/shard_map/reduce_sum | solution.py:43
  20.7 3.1 %fusion.132 = (f32[]{:T(128)}, f32[]{:T(128)}, f32[16,128,128]{2,1,0:T(8,128)S(1)}) fusion(f32[16,128,128]{2,1,0:T(8,128)S(1)} %get-tuple-element.475, f32[16,128]{1,0:T(8,128)S(1)} %bitcast.114, f32[16,128]{1,0:T(8,128)S(1)} %bitcast.138, f32[16,128]{1,0:T(8,128)S(1)} %bitcast.135, f32[16,128]{1,0:T(8,128)S(1)} %bitcast.132, f32[16,128]{1,0:T(8,128)S(1)} %bitcast.123, ...), kind=kLoop, calls=%fused_computation.314 | loop fusion | flops 13107198 | bytes 2162696 | tf_op jit(solution)/shard_map/reduce_sum | solution.py:74
  23.9 7.4 %fusion.160 = (f32[]{:T(128)}, f32[]{:T(128)}, f32[]{:T(128)}, f32[]{:T(128)}, f32[]{:T(128)}, /*index=5*/f32[]{:T(128)}, f32[16,128,128]{2,1,0:T(8,128)S(1)}, f32[16,128,128]{2,1,0:T(8,128)S(1)}, f32[16,128,128]{2,1,0:T(8,128)S(1)}) fusion(f32[16,128,128]{2,1,0:T(8,128)S(1)} %get-tuple-element.471, f32[16,128]{1,0:T(8,128)S(1)} %bitcast.124, ...), kind=kLoop, calls=%fused_computation.342 | loop fusion | flops 39321596 | bytes 6389784 | tf_op jit(solution)/shard_map/reduce_sum | solution.py:74
  31.3 8.2 %multiply_reduce_fusion = (f32[16,128,128]{2,1,0:T(8,128)S(1)}, f32[16,128,128]{2,1,0:T(8,128)S(1)}, f32[3,16,128]{2,1,0:T(8,128)}, f32[3,16,128]{2,1,0:T(8,128)...) fusion(f32[3]{0:T(128)S(1)} %copy-done.11, ...), kind=kLoop, calls=%fused_computation.5 | loop fusion | flops 29061120 | bytes 9756780 | tf_op jit(solution)/shard_map/reduce_sum | solution.py:43
  39.6 7.4 %fusion.146 = (f32[]{:T(128)}, f32[]{:T(128)}, f32[]{:T(128)}, f32[]{:T(128)}, f32[]{:T(128)}, /*index=5*/f32[]{:T(128)}, f32[16,128,128]{2,1,0:T(8,128)S(1)}, f32[16,128,128]{2,1,0:T(8,128)S(1)}, f32[16,128,128]{2,1,0:T(8,128)S(1)}) fusion(f32[16,128,128]{2,1,0:T(8,128)S(1)} %get-tuple-element.470, f32[16,128]{1,0:T(8,128)S(1)} %bitcast.115, ...), kind=kLoop, calls=%fused_computation.328 | loop fusion | flops 39321596 | bytes 6389784 | tf_op jit(solution)/shard_map/reduce_sum | solution.py:74
  47.0 4.8 %rsqrt_multiply_fusion.31 = (f32[16,128,128]{2,1,0:T(8,128)S(1)}, f32[16,128,128]{2,1,0:T(8,128)S(1)}, f32[16,128,128]{2,1,0:T(8,128)S(1)}) fusion(f32[16,128,128]{2,1,0:T(8,128)S(1)} %get-tuple-element.468, f32[16,128]{1,0:T(8,128)S(1)} %bitcast.147, f32[16,128]{1,0:T(8,128)S(1)} %bitcast.144, f32[16,128]{1,0:T(8,128)S(1)} %bitcast.141, ...), kind=kLoop, calls=%fused_computation.241 | loop fusion | flops 27525120 | bytes 6389760 | tf_op jit(solution)/shard_map/mul | solution.py:72
  51.8 9.9 %fusion.4 = (f32[3,16,128]{2,1,0:T(8,128)S(1)}, f32[3,16,128]{2,1,0:T(8,128)S(1)}, f32[16,128,128]{2,1,0:T(8,128)S(1)}, f32[3,16,128]{2,1,0:T(8,128)S(1)}, f32[3...) fusion(f32[16,128,128]{2,1,0:T(8,128)S(1)} %get-tuple-element.5, ...), kind=kLoop, calls=%fused_computation.8 | loop fusion | flops 31383552 | bytes 9879636 | tf_op jit(solution)/shard_map/reduce_sum | solution.py:74
  61.7 4.9 %fusion.167 = (f32[]{:T(128)}, f32[]{:T(128)}, f32[]{:T(128)}, f32[]{:T(128)}, f32[16,128,128]{2,1,0:T(8,128)S(1)}) fusion(f32[16,128,128]{2,1,0:T(8,128)S(1)} %get-tuple-element.459, f32[16,128]{1,0:T(8,128)S(1)} %bitcast.148, f32[16,128]{1,0:T(8,128)S(1)} %bitcast.145, f32[16,128]{1,0:T(8,128)S(1)} %bitcast.142, f32[16,128]{1,0:T(8,128)S(1)} %bitcast.130, ...), kind=kLoop, calls=%fused_computation.349 | loop fusion | flops 23855100 | bytes 4292624 | tf_op jit(solution)/shard_map/reduce_sum | solution.py:74
  66.6 7.0 %fusion.153 = (f32[]{:T(128)}, f32[]{:T(128)}, f32[]{:T(128)}, f32[]{:T(128)}, f32[]{:T(128)}, /*index=5*/f32[]{:T(128)}, f32[16,128,128]{2,1,0:T(8,128)S(1)}, f32[16,128,128]{2,1,0:T(8,128)S(1)}) fusion(f32[16,128,128]{2,1,0:T(8,128)S(1)} %get-tuple-element.460, f32[16,128]{1,0:T(8,128)S(1)} %bitcast.125, f32[16,128]{1,0:T(8,128)S(1)} %bitcast.122, ...), kind=kLoop, calls=%fused_computation.335 | loop fusion | flops 37224444 | bytes 6455320 | tf_op jit(solution)/shard_map/reduce_sum | solution.py:74
  73.6 4.6 %fusion.125 = (f32[]{:T(128)}, f32[]{:T(128)}, f32[]{:T(128)}, f32[]{:T(128)}, f32[16,128,128]{2,1,0:T(8,128)S(1)}) fusion(f32[16,128,128]{2,1,0:T(8,128)S(1)} %get-tuple-element.457, f32[16,128]{1,0:T(8,128)S(1)} %bitcast.192, f32[16,128]{1,0:T(8,128)S(1)} %bitcast.193, f32[16,128]{1,0:T(8,128)S(1)} %bitcast.194, f32[16,128]{1,0:T(8,128)S(1)} %bitcast.191, ...), kind=kLoop, calls=%fused_computation.307 | loop fusion | flops 23855100 | bytes 4292624 | tf_op jit(solution)/shard_map/reduce_sum | solution.py:74
  78.2 3.0 %fusion.22 = (f32[3,16,128]{2,1,0:T(8,128)S(1)}, f32[3,16,128]{2,1,0:T(8,128)S(1)}, f32[3,16,128]{2,1,0:T(8,128)S(1)}, f32[3,16,128]{2,1,0:T(8,128)S(1)}) fusion(f32[16,128,128]{2,1,0:T(8,128)S(1)} %get-tuple-element.491, f32[3,16,128]{2,1,0:T(8,128)S(1)} %bitcast.107, f32[3,16,128]{2,1,0:T(8,128)S(1)} %bitcast.82, f32[16,128,128]{2,1,0:T(8,128)S(1)} %get-tuple-element.499), kind=kLoop, calls=%fused_computation.38 | loop fusion | flops 7053312 | bytes 2244608 | tf_op jit(solution)/shard_map/reduce_sum | solution.py:74
  81.3 0.6 neg.108
  82.2 0.2 scatter-add.119
  82.4 0.8 fusion.319
  83.2 0.8 slice_add_fusion.16
  84.0 0.2 scatter-add.121
  84.3 0.2 scatter-add.125
  84.5 0.2 scatter-add.129
  84.8 5.0 %fusion.10 = (f32[3,16,128]{2,1,0:T(8,128)S(1)}, f32[3,16,128]{2,1,0:T(8,128)S(1)}, f32[3,16,128]{2,1,0:T(8,128)S(1)}, f32[3,16,128]{2,1,0:T(8,128)S(1)}, f32[3,...) fusion(f32[16,128,128]{2,1,0:T(8,128)S(1)} %get-tuple-element.498, f32[3]{0:T(128)S(1)} %copy-done.12, ...), kind=kLoop, calls=%fused_computation.18 | loop fusion | flops 11759616 | bytes 3366948 | tf_op jit(solution)/shard_map/reduce_sum | solution.py:74
  89.9 0.2 scatter-add.135
  90.2 0.2 scatter-add.139
  90.5 0.2 scatter-add.141
  90.8 0.2 scatter-add.145
  91.1 0.2 scatter-add.149
  91.4 0.4 collective-permute-start.3
  91.8 5.6 %collective-permute-done.3 = f32[3,3,5,1,128]{4,3,2,1,0:T(1,128)S(1)} collective-permute-done((f32[3,3,5,1,128]{4,3,2,1,0:T(1,128)S(1)}, f32[3,3,5,1,128]{4,3,2,1,0:T(1,128)S(1)}, u32[]{:S(2)}, u32[]{:S(2)}) %collective-permute-start.3) | collective-permute-done | bytes 23072 | tf_op jit(solution)/shard_map/ppermute | solution.py:18
  97.4 0.1 scatter-add.150
  97.6 0.1 collective-permute-start.4
  115.2 16.3 %all-reduce.1 = (f32[]{:T(128)}, f32[]{:T(128)}) all-reduce(f32[]{:T(128)S(6)} %add.995, f32[]{:T(128)S(6)} %add.982), channel_id=1, replica_groups=mesh['gx'=4,'gy'=2,'gz'=4] {'gy','gz'}, use_global_device_ids=true, to_apply=%region_75.0 | all-reduce | flops 2 | bytes 16 | tf_op jit(solution)/shard_map/psum | solution.py:124
  131.6 11.4 %all-reduce.2 = (f32[1]{0:T(128)}, f32[1]{0:T(128)}) all-reduce(f32[1]{0:T(128)} %bitcast.71, f32[1]{0:T(128)} %bitcast.70), channel_id=1, replica_groups=mesh['gx'=4,'gy'=2,'gz'=4] {'gx'}, use_global_device_ids=true, to_apply=%region_76.0 | all-reduce | flops 2 | bytes 16 | tf_op jit(solution)/shard_map/psum | solution.py:124
  143.0 1.9 %maximum_multiply_fusion = f32[2]{0:T(128)} fusion(f32[1]{0:T(128)} %get-tuple-element.487, f32[1]{0:T(128)} %get-tuple-element.488), kind=kLoop, calls=%fused_computation.665 | loop fusion | flops 4 | bytes 16 | tf_op jit(solution)/shard_map/mul | solution.py:134
  144.9 2.7 %collective-permute-done.5 = f32[3,1,4,2,128]{4,3,2,1,0:T(2,128)S(1)} collective-permute-done((f32[3,1,4,2,128]{4,3,2,1,0:T(2,128)S(1)}, f32[3,1,4,2,128]{4,3,2,1,0:T(2,128)S(1)}, u32[]{:S(2)}, u32[]{:S(2)}) %collective-permute-start.5) | collective-permute-done | bytes 12320 | tf_op jit(solution)/shard_map/ppermute | solution.py:18
  147.6 0.6 copy-done.3
  (101 shorter events, 1.4 us)
Async XLA Ops:
  0.6 16.4 %copy-start.5 = (f32[3]{0:T(128)S(1)}, f32[3]{0:T(128)}, u32[]{:S(2)}) copy-start(f32[3]{0:T(128)} %constant.879.clone) | copy-start | bytes 40
  0.6 16.4 %copy-start.13 = (f32[3]{0:T(128)S(1)}, f32[3]{0:T(128)}, u32[]{:S(2)}) copy-start(f32[3]{0:T(128)} %constant.880.clone) | copy-start | bytes 40
  0.7 16.4 %copy-start.14 = (f32[3]{0:T(128)S(1)}, f32[3]{0:T(128)}, u32[]{:S(2)}) copy-start(f32[3]{0:T(128)} %constant.883.clone) | copy-start | bytes 40
  0.7 16.4 %copy-start.6 = (f32[3]{0:T(128)S(1)}, f32[3]{0:T(128)}, u32[]{:S(2)}) copy-start(f32[3]{0:T(128)} %constant.886.clone) | copy-start | bytes 40
  0.7 16.4 %copy-start.15 = (f32[3]{0:T(128)S(1)}, f32[3]{0:T(128)}, u32[]{:S(2)}) copy-start(f32[3]{0:T(128)} %constant.890.clone) | copy-start | bytes 40
  0.7 16.4 %copy-start = (f32[3,2,4,2,128]{4,3,2,1,0:T(2,128)S(1)}, f32[3,2,4,2,128]{4,3,2,1,0:T(2,128)}, u32[]{:S(2)}) copy-start(f32[3,2,4,2,128]{4,3,2,1,0:T(2,128)} %param.82) | copy-start | bytes 73732
  4.5 5.5 %collective-permute-start = (f32[7,1,4,2,128]{4,3,2,1,0:T(2,128)S(1)}, f32[7,1,4,2,128]{4,3,2,1,0:T(2,128)S(1)}, u32[]{:S(2)}, u32[]{:S(2)}) collective-permute-start(f32[7,1,4,2,128]{4,3,2,1,0:T(2,128)S(1)} %slice.1661), channel_id=1, source_target_pairs={{0,24},{8,0},{16,8},{24,16},{1,25},{9,1},{17,9},{25,17},{2,26},{10... | collective-permute-start | bytes 86024 | tf_op jit(solution)/shard_map/ppermute | solution.py:18
  10.1 1.3 collective-permute-start.1
  11.4 5.5 %collective-permute-start.2 = (f32[7,3,5,1,128]{4,3,2,1,0:T(1,128)S(1)}, f32[7,3,5,1,128]{4,3,2,1,0:T(1,128)S(1)}, u32[]{:S(2)}, u32[]{:S(2)}) collective-permute-start(f32[7,3,5,1,128]{4,3,2,1,0:T(1,128)S(1)} %slice.1680), channel_id=1, source_target_pairs={{0,3},{1,0},{2,1},{3,2},{4,7},{5,4},{6,5},{7,6},{8,11},{9,8},{10,9... | collective-permute-start | bytes 161288 | tf_op jit(solution)/shard_map/ppermute | solution.py:18
  23.8 7.5 %copy-start.7 = (f32[3]{0:T(128)S(1)}, f32[3]{0:T(128)}, u32[]{:S(2)}) copy-start(f32[3]{0:T(128)} %constant.881.clone) | copy-start | bytes 40
  23.8 7.5 %copy-start.8 = (f32[3]{0:T(128)S(1)}, f32[3]{0:T(128)}, u32[]{:S(2)}) copy-start(f32[3]{0:T(128)} %constant.882.clone) | copy-start | bytes 40
  23.8 7.4 %copy-start.9 = (f32[3]{0:T(128)S(1)}, f32[3]{0:T(128)}, u32[]{:S(2)}) copy-start(f32[3]{0:T(128)} %constant.884.clone) | copy-start | bytes 40
  23.9 7.4 %copy-start.10 = (f32[3]{0:T(128)S(1)}, f32[3]{0:T(128)}, u32[]{:S(2)}) copy-start(f32[3]{0:T(128)} %constant.888.clone) | copy-start | bytes 40
  23.9 7.4 %copy-start.11 = (f32[3]{0:T(128)S(1)}, f32[3]{0:T(128)}, u32[]{:S(2)}) copy-start(f32[3]{0:T(128)} %constant.891.clone) | copy-start | bytes 40
  23.9 7.4 %copy-start.12 = (f32[3]{0:T(128)S(1)}, f32[3]{0:T(128)}, u32[]{:S(2)}) copy-start(f32[3]{0:T(128)} %constant.889.clone) | copy-start | bytes 40
  47.0 4.8 %copy-start.4 = (f32[3]{0:T(128)S(1)}, f32[3]{0:T(128)}, u32[]{:S(2)}) copy-start(f32[3]{0:T(128)} %constant.887.clone) | copy-start | bytes 40
  84.8 6.0 %copy-start.1 = (f32[3,16,128]{2,1,0:T(8,128)S(1)}, f32[3,16,128]{2,1,0:T(8,128)}, u32[]{:S(2)}) copy-start(f32[3,16,128]{2,1,0:T(8,128)} %get-tuple-element.462) | copy-start | bytes 73732
  84.8 6.0 %copy-start.2 = (f32[3,16,128]{2,1,0:T(8,128)S(1)}, f32[3,16,128]{2,1,0:T(8,128)}, u32[]{:S(2)}) copy-start(f32[3,16,128]{2,1,0:T(8,128)} %get-tuple-element.461) | copy-start | bytes 73732
  91.4 6.0 %collective-permute-start.3 = (f32[3,3,5,1,128]{4,3,2,1,0:T(1,128)S(1)}, f32[3,3,5,1,128]{4,3,2,1,0:T(1,128)S(1)}, u32[]{:S(2)}, u32[]{:S(2)}) collective-permute-start(f32[3,3,5,1,128]{4,3,2,1,0:T(1,128)S(1)} %slice.1705), channel_id=1, source_target_pairs={{0,1},{1,2},{2,3},{3,0},{4,5},{5,6},{6,7},{7,4},{8,9},{9,10},{10,1... | collective-permute-start | bytes 69128 | tf_op jit(solution)/shard_map/ppermute | solution.py:18
  97.6 45.4 %collective-permute-start.4 = (f32[3,3,1,2,128]{4,3,2,1,0:T(2,128)S(1)}, f32[3,3,1,2,128]{4,3,2,1,0:T(2,128)S(1)}, u32[]{:S(2)}, u32[]{:S(2)}) collective-permute-start(f32[3,3,1,2,128]{4,3,2,1,0:T(2,128)S(1)} %slice.1708), channel_id=1, source_target_pairs={{0,4},{4,0},{1,5},{5,1},{2,6},{6,2},{3,7},{7,3},{8,12},{12,8},{9,1... | collective-permute-start | bytes 27656 | tf_op jit(solution)/shard_map/ppermute | solution.py:18
  142.9 4.6 %collective-permute-start.5 = (f32[3,1,4,2,128]{4,3,2,1,0:T(2,128)S(1)}, f32[3,1,4,2,128]{4,3,2,1,0:T(2,128)S(1)}, u32[]{:S(2)}, u32[]{:S(2)}) collective-permute-start(f32[3,1,4,2,128]{4,3,2,1,0:T(2,128)S(1)} %slice.1711), channel_id=1, source_target_pairs={{0,8},{8,16},{16,24},{24,0},{1,9},{9,17},{17,25},{25,1},{2,10},{10... | collective-permute-start | bytes 36872 | tf_op jit(solution)/shard_map/ppermute | solution.py:18
  147.6 0.6 copy-start.3
